TPU v7x, 16 devices: a whole 2x2x2 slice. The times are simulated.
16 devices in a mesh: dp: 1, tp: 16 (over x, y, z, core).
Axes of the slice: x: 2, y: 2, z: 2, core: 2. Of those that a mesh axis runs over, the one named last changes fastest.
Arguments:
- x: bfloat16 [2048, 4096], P('dp')
- dy: bfloat16 [2048, 4096], P('dp')
- gate: bfloat16 [2048, 12288], P('dp', 'tp')
- up: bfloat16 [2048, 12288], P('dp', 'tp')
- w_gate: bfloat16 [4096, 12288], P(None, 'tp')
- w_up: bfloat16 [4096, 12288], P(None, 'tp')
- w_down: bfloat16 [12288, 4096], P('tp')
Outputs:
- output 1: bfloat16 [2048, 4096], P('dp')
- output 2: bfloat16 [4096, 12288], P('dp', 'tp')
- output 3: bfloat16 [4096, 12288], P('dp', 'tp')
- output 4: bfloat16 [12288, 4096], P(('dp', 'tp'))
All inputs are finite; a program needn't handle non-finite values.
Results may differ from a plain program's by a relative error of at most 0.012.
Values are sent between devices in bfloat16 or wider.
A program may use at most 2 GiB of HBM per device.

v0:
```python
import jax
import jax.numpy as jnp
from jax import lax
from jax.sharding import PartitionSpec as P


def act(gate, up):
    return jax.nn.silu(gate) * up


def solution(mesh):
    def step(x, dy, gate, up, w_gate, w_up, w_down):
        hidden, back = jax.vjp(act, gate.astype(jnp.float32), up.astype(jnp.float32))
        d_hidden = jnp.dot(dy, w_down.T, preferred_element_type=jnp.float32)
        d_gate, d_up = (g.astype(jnp.bfloat16) for g in back(d_hidden))
        term = jnp.dot(d_gate, w_gate.T, preferred_element_type=jnp.float32) + jnp.dot(d_up, w_up.T, preferred_element_type=jnp.float32)
        dx = lax.psum(term.astype(jnp.bfloat16), "tp")
        dw_gate = jnp.dot(x.T, d_gate, preferred_element_type=jnp.float32)
        dw_up = jnp.dot(x.T, d_up, preferred_element_type=jnp.float32)
        dw_down = jnp.dot(hidden.astype(jnp.bfloat16).T, dy, preferred_element_type=jnp.float32)
        return dx, *(g.astype(jnp.bfloat16) for g in (dw_gate, dw_up, dw_down))

    tokens, columns, rows = P("dp", None), P(None, "tp"), P("tp", None)
    return jax.shard_map(
        step,
        mesh=mesh,
        in_specs=(tokens, tokens, P("dp", "tp"), P("dp", "tp"), columns, columns, rows),
        out_specs=(tokens, P("dp", "tp"), P("dp", "tp"), P(("dp", "tp"), None)),
        check_vma=False,
    )
```

profile of v0, /device:TPU:0, one launch (start us, length us, event | category | flops | bytes accessed | tf_op | source)
XLA Modules:
  0.0 283.0 jit_solution(4024521221218289855)
XLA Ops:
  7.2 0.0 all-reduce.2.cloned.1.call-start
  7.2 23.6 %fusion.6 = (bf16[2048,768]{1,0:T(8,128)(2,1)}, f32[2048,768]{1,0:T(8,128)}) fusion(bf16[2048,768]{1,0:T(8,128)(2,1)} %param.9, bf16[2048,768]{1,0:T(8,128)(2,1)} %param.10, bf16[2048,4096]{1,0:T(8,128)(2,1)} %param.8, bf16[768,4096]{1,0:T(8,128)(2,1)} %param.13), kind=kOutput, calls=%fused_computation.16 | convolution fusion | flops 12905349120 | bytes 38797312 | tf_op jit(solution)/shard_map/dot_general | solution.py:14
  30.8 0.0 copy-start
  30.8 22.3 %fusion.11 = f32[2048,4096]{1,0:T(8,128)} fusion(bf16[2048,768]{1,0:T(8,128)(2,1)} %get-tuple-element.8, bf16[4096,768]{1,0:T(8,128)(2,1)} %param.11), kind=kOutput, calls=%fused_computation.21 | convolution fusion | flops 12884901888 | bytes 42991616 | tf_op jit(solution)/shard_map/dot_general | solution.py:16
  53.1 0.0 copy-done
  53.1 26.2 %add_convert_fusion = bf16[2048,4096]{1,0:T(8,128)(2,1)} fusion(f32[2048,4096]{1,0:T(8,128)} %fusion.11, bf16[4096,768]{1,0:T(8,128)(2,1)} %param.12, f32[2048,768]{1,0:T(8,128)} %get-tuple-element.9, bf16[2048,768]{1,0:T(8,128)(2,1)S(1)} %copy-done), kind=kOutput, calls=%fused_computation | convolution fusion | flops 12912689152 | bytes 66060288 | tf_op jit(solution)/shard_map/dot_general | solution.py:16
  79.3 0.0 all-reduce.2.cloned.1.call-update
  79.3 19.5 %fusion.7 = bf16[4096,768]{0,1:T(8,128)(2,1)} fusion(bf16[2048,768]{1,0:T(8,128)(2,1)} %get-tuple-element.8, bf16[2048,4096]{1,0:T(8,128)(2,1)} %param.7), kind=kOutput, calls=%fused_computation.18 | convolution fusion | flops 12888047616 | bytes 26214400 | tf_op jit(solution)/shard_map/dot_general | solution.py:18
  98.8 8.6 %copy.11 = bf16[4096,768]{1,0:T(8,128)(2,1)} copy(bf16[4096,768]{0,1:T(8,128)(2,1)} %fusion.7) | data formatting | bytes 12582912
  107.4 21.2 %fusion.8 = bf16[4096,768]{0,1:T(8,128)(2,1)} fusion(bf16[2048,4096]{1,0:T(8,128)(2,1)} %param.7, f32[2048,768]{1,0:T(8,128)} %get-tuple-element.9, bf16[2048,768]{1,0:T(8,128)(2,1)S(1)} %copy-done), kind=kOutput, calls=%fused_computation.19 | convolution fusion | flops 12899057664 | bytes 32505856 | tf_op jit(solution)/shard_map/dot_general | solution.py:19
  128.6 8.6 %copy.12 = bf16[4096,768]{1,0:T(8,128)(2,1)} copy(bf16[4096,768]{0,1:T(8,128)(2,1)} %fusion.8) | data formatting | bytes 12582912
  137.2 21.2 %convolution_convert_fusion = bf16[768,4096]{1,0:T(8,128)(2,1)} fusion(bf16[2048,4096]{1,0:T(8,128)(2,1)} %param.8, bf16[2048,768]{1,0:T(8,128)(2,1)} %param.10, bf16[2048,768]{1,0:T(8,128)(2,1)S(1)} %copy-done), kind=kOutput, calls=%fused_computation.7 | convolution fusion | flops 12900630528 | bytes 29360128 | tf_op jit(solution)/shard_map/dot_general | solution.py:20
  158.4 103.7 %all-reduce.2.cloned.1.call-done = bf16[2048,4096]{1,0:T(8,128)(2,1)} async-done(((bf16[2048,4096]{1,0:T(8,128)(2,1)}), bf16[2048,4096]{1,0:T(8,128)(2,1)}) %all-reduce.2.cloned.1.call-update) | async-done | bytes 16777232 | tf_op jit(solution)/shard_map/psum | solution.py:17
  262.1 14.1 %copy.14 = bf16[2048,4096]{1,0:T(8,128)(2,1)} copy(bf16[2048,4096]{1,0:T(8,128)(2,1)} %all-reduce.2.cloned.1.call-done) | data formatting | bytes 33554432
Async XLA Ops:
  7.2 254.9 %all-reduce.2.cloned.1.call-start = ((), (), s32[]{:S(2)}) async-start(), calls=%async_computation | async-start | bytes 33554432 | tf_op jit(solution)/shard_map/psum | solution.py:17
  30.8 22.3 %copy-start = (bf16[2048,768]{1,0:T(8,128)(2,1)S(1)}, bf16[2048,768]{1,0:T(8,128)(2,1)}, u32[]{:S(2)}) copy-start(bf16[2048,768]{1,0:T(8,128)(2,1)} %param.9) | copy-start | bytes 9437188
Sparse Core Ops, SparseCore 0:
  79.4 182.6 all-reduce.1
where the time goes:
time: 284 us; the launch traced here: 283 us
  matrix products  134 us (47%)
  waiting for transfers between devices  104 us (37%)
  local copies, waits for them, and re-layouts  31.3 us (11%)
  between operations  14 us (5%)
    psum x1, waiting for transfers between devices, step(): dx = lax.psum(term.astype(jnp.bfloat16), 'tp')  104 us
    unnamed x5, local copies, waits for them, and re-layouts  31.3 us
    dot_general x1, matrix products, step(): jnp.dot(d_up, w_up.T, preferred_element_type=jnp.float32)  26.2 us
    dot_general x1, matrix products, step(): d_hidden = jnp.dot(dy, w_down.T, preferred_element_type=jnp.float32)  23.6 us
    dot_general x1, matrix products, step(): jnp.dot(d_gate, w_gate.T, preferred_element_type=jnp.float32)  22.3 us
    dot_general x1, matrix products, step(): dw_up = jnp.dot(x.T, d_up, preferred_element_type=jnp.float32)  21.2 us
    dot_general x1, matrix products, step(): jnp.dot(hidden.astype(jnp.bfloat16).T, dy, preferred_element_type=jnp.flo...  21.2 us
    dot_general x1, matrix products, step(): dw_gate = jnp.dot(x.T, d_gate, preferred_element_type=jnp.float32)  19.5 us
  transfers between devices with their start and end apart: 1, of which 1 were waited for; matrix products, arithmetic and copies ran while one was open for 28% of the time, Pallas kernels for 0%

commit v1 on v0

v1 whole, which is shorter than its diff:
```python
import jax
import jax.numpy as jnp
from jax import lax
from jax.experimental import pallas as pl
from jax.experimental.pallas import tpu as pltpu
from jax.sharding import PartitionSpec as P

bf16, f32 = jnp.bfloat16, jnp.float32
MESH = pl.DeviceIdType.MESH
ROWS, D, FF = 2048, 4096, 768
CHUNKS, R = 8, 256
HALF = D // 2
OFF, WIDTH = (0, 768, 1536), (768, 768, 512)
GROUPS = range(3)
TILE = 256
NB = 1024
AG3 = ((0, 1, 2), (3, 4), (5,), (6,), (7,), (), (), ())
AG2 = ((), (0, 1), (2,), (3,), (4,), (5, 6), (7,), ())
AG1 = ((), (), (), (0,), (1,), (2,), (3,), (4,))


def dot(a, b, ca, cb):
    return lax.dot_general(a, b, (((ca,), (cb,)), ((), ())), preferred_element_type=f32)


def kernel(
    x, dy, gate, up, wg, wu, wd,
    dx, dwg, dwu, dwd,
    dg, du, hid, dyb, ring, acc, kp1, kp2, s1, s2, s3, r1, r2, r3,
    dy_sem, w_sem, xd_sem, ss, rs, free,
):
    me = lax.axis_index("tp")
    core = lax.rem(me, 2)
    bits = tuple(lax.rem(me // s, 2) for s in (8, 4, 2))
    other = me + 1 - 2 * core

    def pick(r, values):
        return jnp.where(r == 0, values[0], jnp.where(r == 1, values[1], values[2]))

    peers = tuple(me + s * (1 - 2 * b) for s, b in zip((8, 4, 2), bits))

    def chunk_copies(k):
        rows = pl.ds(pl.multiple_of(k * R, R), R)
        return [
            pltpu.make_async_copy(dy.at[rows, :], dyb, dy_sem.at[0]),
            pltpu.make_async_copy(gate.at[rows, :], hid.at[rows, :], dy_sem.at[1]),
            pltpu.make_async_copy(up.at[rows, :], du.at[rows, :], dy_sem.at[2]),
        ]

    def w_copies(half, i):
        rows = pl.ds(pl.multiple_of(half * HALF, HALF), HALF)
        return [pltpu.make_async_copy(a.at[rows, :], b.at[rows, :], w_sem.at[i, n]) for n, (a, b) in enumerate(((wg, dwg), (wu, dwu)))]

    def xd_copy(t, which):
        i = 2 * t + which
        cols = pl.ds(pl.multiple_of(t * TILE, TILE), TILE)
        return pltpu.make_async_copy((x, dy)[which].at[:, cols], ring.at[lax.rem(i, 3)], xd_sem.at[lax.rem(i, 3)])

    wd_copy = pltpu.make_async_copy(wd, dwd, w_sem.at[2, 0])
    first = chunk_copies(0)
    first[0].start()
    wd_copy.start()
    first[1].start()
    first[2].start()
    for c in w_copies(1 - core, 0) + w_copies(core, 1):
        c.start()

    barrier = pltpu.get_barrier_semaphore()
    for p in peers + (other,):
        pl.semaphore_signal(barrier, inc=1, device_id={"tp": p}, device_id_type=MESH)
    pl.semaphore_wait(barrier, 4)

    def remote(kind, k, g, src, dst, to):
        return pltpu.make_async_remote_copy(
            src_ref=src, dst_ref=dst, send_sem=ss.at[kind, k, g], recv_sem=rs.at[kind, k, g],
            device_id={"tp": to}, device_id_type=MESH,
        )

    def place(k, g):
        o = [lax.rem(g + k + i, 3) for i in range(3)]
        b = [pick(r, bits) for r in o]
        p = [pick(r, peers) for r in o]
        keep1 = k * R + b[0] * 128
        send1 = k * R + (1 - b[0]) * 128
        keep2, send2 = keep1 + b[1] * 64, keep1 + (1 - b[1]) * 64
        keep3, send3 = keep2 + b[2] * 32, keep2 + (1 - b[2]) * 32
        return b, p, (keep1, keep2, keep3), (send1, send2, send3)

    def mine(start, n, g):
        return dx.at[pl.ds(pl.multiple_of(start, 32), n), pl.ds(pl.multiple_of(core * HALF + OFF[g], 256), WIDTH[g])]

    def theirs(k, g):
        return dx.at[pl.ds(pl.multiple_of(k * R, R), R), pl.ds(pl.multiple_of((1 - core) * HALF + OFF[g], 256), WIDTH[g])]

    def copy_of(kind, k, g):
        b, p, keep, send = place(k, g)
        cols = pl.ds(OFF[g], WIDTH[g])
        if kind == 0:
            return remote(0, k, g, theirs(k, g), theirs(k, g), other)
        if kind == 1:
            return remote(1, k, g, s1.at[:, cols], r1.at[k, :, cols], p[0])
        if kind == 2:
            return remote(2, k, g, s2.at[:, cols], r2.at[k, :, cols], p[1])
        if kind == 3:
            return remote(3, k, g, s3.at[:, cols], r3.at[k, :, cols], p[2])
        if kind == 4:
            return remote(4, k, g, mine(keep[2], 32, g), mine(keep[2], 32, g), p[2])
        if kind == 5:
            return remote(5, k, g, mine(keep[1], 64, g), mine(keep[1], 64, g), p[1])
        if kind == 6:
            return remote(6, k, g, mine(keep[0], 128, g), mine(keep[0], 128, g), p[0])
        if kind == 7:
            return remote(7, k, g, mine(keep[1], 64, g), mine(keep[1], 64, g), other)
        if kind == 8:
            return remote(8, k, g, mine(send[1], 64, g), mine(send[1], 64, g), other)
        return remote(9, k, g, mine(send[0], 128, g), mine(send[0], 128, g), other)

    def slot_of(k):
        return lax.rem(k, 2)

    def sent(kind, k, g):
        @pl.when(k >= 1)
        def _():
            copy_of(kind, k - 1, g).wait_send()

    def after_own(k, g):
        b, p, keep, send = place(k, g)
        s, cols, w = slot_of(k), pl.ds(OFF[g], WIDTH[g]), WIDTH[g]
        copy_of(0, k, g).wait_recv()
        sent(1, k, g)
        for i in range(0, 128, 32):
            v = acc[pl.ds(pl.multiple_of((1 - b[0]) * 128 + i, 32), 32), cols]
            s1[pl.ds(i, 32), cols] = (v + mine(send[0] + i, 32, g)[...].astype(f32)).astype(bf16)
        copy_of(1, k, g).start()
        for i in range(0, 128, 32):
            v = acc[pl.ds(pl.multiple_of(b[0] * 128 + i, 32), 32), cols]
            kp1[s, pl.ds(i, 32), cols] = v + mine(keep[0] + i, 32, g)[...].astype(f32)

    def rs1(k, g):
        b, p, keep, send = place(k, g)
        s, cols = slot_of(k), pl.ds(OFF[g], WIDTH[g])
        copy_of(1, k, g).wait_recv()
        sent(2, k, g)
        for i in range(0, 64, 32):
            rows = pl.ds(pl.multiple_of((1 - b[1]) * 64 + i, 32), 32)
            s2[pl.ds(i, 32), cols] = (kp1[s, rows, cols] + r1[k, rows, cols].astype(f32)).astype(bf16)
        copy_of(2, k, g).start()
        for i in range(0, 64, 32):
            rows = pl.ds(pl.multiple_of(b[1] * 64 + i, 32), 32)
            kp2[s, pl.ds(i, 32), cols] = kp1[s, rows, cols] + r1[k, rows, cols].astype(f32)

    def rs2(k, g):
        b, p, keep, send = place(k, g)
        s, cols = slot_of(k), pl.ds(OFF[g], WIDTH[g])
        copy_of(2, k, g).wait_recv()
        sent(3, k, g)
        there = pl.ds(pl.multiple_of((1 - b[2]) * 32, 32), 32)
        here = pl.ds(pl.multiple_of(b[2] * 32, 32), 32)
        s3[:, cols] = (kp2[s, there, cols] + r2[k, there, cols].astype(f32)).astype(bf16)
        copy_of(3, k, g).start()
        kp2[s, here, cols] = kp2[s, here, cols] + r2[k, here, cols].astype(f32)

    def rs3(k, g):
        b, p, keep, send = place(k, g)
        s, cols = slot_of(k), pl.ds(OFF[g], WIDTH[g])
        copy_of(3, k, g).wait_recv()
        here = pl.ds(pl.multiple_of(b[2] * 32, 32), 32)
        mine(keep[2], 32, g)[...] = (kp2[s, here, cols] + r3[k, :, cols].astype(f32)).astype(bf16)
        copy_of(4, k, g).start()

    def ag3(k, g):
        copy_of(4, k, g).wait_recv()
        copy_of(5, k, g).start()
        copy_of(7, k, g).start()

    def ag2(k, g):
        copy_of(5, k, g).wait_recv()
        copy_of(6, k, g).start()
        copy_of(8, k, g).start()

    def ag1(k, g):
        copy_of(6, k, g).wait_recv()
        copy_of(9, k, g).start()

    def all_groups(event, k):
        if event is ag3:
            pl.semaphore_wait(free.at[k], 1)
        for g in GROUPS:
            event(k, g)

    def halving(k):
        @pl.when(jnp.logical_and(k >= 3, k < 11))
        def _():
            all_groups(rs3, k - 3)

        @pl.when(jnp.logical_and(k >= 2, k < 10))
        def _():
            all_groups(rs2, k - 2)

        @pl.when(jnp.logical_and(k >= 1, k < 9))
        def _():
            all_groups(rs1, k - 1)

    wd_copy.wait()

    @pl.loop(0, CHUNKS)
    def _(k):
        rows = pl.ds(pl.multiple_of(k * R, R), R)
        for c in chunk_copies(k):
            c.wait()
        acc[:, pl.ds(0, FF)] = dot(dyb[...], dwd[...], 1, 1)

        @pl.loop(0, R // 16)
        def _(i):
            block = pl.ds(pl.multiple_of(i * 16, 16), 16)
            here = pl.ds(pl.multiple_of(k * R + i * 16, 16), 16)
            a, b, d = hid[here, :].astype(f32), du[here, :].astype(f32), acc[block, pl.ds(0, FF)]
            sig = jax.nn.sigmoid(a)
            silu = a * sig
            hid[here, :] = (silu * b).astype(bf16)
            du[here, :] = (d * silu).astype(bf16)
            dg[here, :] = (d * b * (sig + silu * (1.0 - sig))).astype(bf16)

        @pl.when(k < CHUNKS - 1)
        def _():
            for c in chunk_copies(k + 1):
                c.start()

        @pl.when(k == CHUNKS - 1)
        def _():
            for i in range(3):
                xd_copy(i // 2, i % 2).start()

        @pl.when(k == 0)
        def _():
            for c in w_copies(1 - core, 0):
                c.wait()

        for n in range(0, HALF, NB):
            w = pl.ds(pl.multiple_of((1 - core) * HALF + n, 256), NB)
            acc[:, pl.ds(n, NB)] = dot(dg[rows, :], dwg[w, :], 1, 1) + dot(du[rows, :], dwu[w, :], 1, 1)
        for g in GROUPS:
            ref = theirs(k, g)
            for i in range(0, R, 32):
                ref[pl.ds(i, 32), :] = acc[pl.ds(i, 32), pl.ds(OFF[g], WIDTH[g])].astype(bf16)
            copy_of(0, k, g).start()

        @pl.when(k == 0)
        def _():
            for c in w_copies(core, 1):
                c.wait()

        for n in range(0, HALF, NB):
            w = pl.ds(pl.multiple_of(core * HALF + n, 256), NB)
            acc[:, pl.ds(n, NB)] = dot(dg[rows, :], dwg[w, :], 1, 1) + dot(du[rows, :], dwu[w, :], 1, 1)
        for g in GROUPS:
            after_own(k, g)

        for g in GROUPS:
            copy_of(0, k, g).wait_send()
        pl.semaphore_signal(free.at[k], inc=1, device_id={"tp": other}, device_id_type=MESH)
        halving(k)

    @pl.loop(0, 8)
    def _(u):
        for s in range(2):
            t = 2 * u + s
            tile = pl.ds(pl.multiple_of(t * TILE, TILE), TILE)
            xd_copy(t, 0).wait()
            xt, yt = ring.at[lax.rem(2 * t, 3)], ring.at[lax.rem(2 * t + 1, 3)]
            dwg[tile, :] = dot(xt[...], dg[...], 0, 0).astype(bf16)
            if s == 0:
                halving(8 + u)
            dwu[tile, :] = dot(xt[...], du[...], 0, 0).astype(bf16)

            @pl.when(t < 15)
            def _():
                xd_copy(t + 1, 1).start()

            xd_copy(t, 1).wait()
            if s == 1:
                for i in range(8):
                    if AG3[i] + AG2[i] + AG1[i]:
                        @pl.when(u == i)
                        def _():
                            for k in AG3[i]:
                                all_groups(ag3, k)
                            for k in AG2[i]:
                                all_groups(ag2, k)
                            for k in AG1[i]:
                                all_groups(ag1, k)
            dwd[:, tile] = dot(hid[...], yt[...], 0, 0).astype(bf16)

            @pl.when(t < 14)
            def _():
                xd_copy(t + 2, 0).start()

    for k in range(5, 8):
        all_groups(ag1, k)

    @pl.loop(0, CHUNKS)
    def _(k):
        for g in GROUPS:
            for kind in range(4, 10):
                if kind >= 7:
                    copy_of(kind, k, g).wait_recv()
                copy_of(kind, k, g).wait_send()

    for g in GROUPS:
        for kind in range(1, 4):
            copy_of(kind, CHUNKS - 1, g).wait_send()


def solution(mesh):
    hbm = pl.BlockSpec(memory_space=pltpu.HBM)
    vmem = pl.BlockSpec(memory_space=pltpu.VMEM)
    sem = pltpu.SemaphoreType.DMA

    def step(*args):
        return tuple(pl.pallas_call(
            kernel,
            out_shape=[pltpu.VMEM(s, bf16) for s in ((ROWS, D), (D, FF), (D, FF), (FF, D))],
            in_specs=[hbm] * 7,
            out_specs=[vmem] * 4,
            scratch_shapes=[
                pltpu.VMEM((ROWS, FF), bf16),
                pltpu.VMEM((ROWS, FF), bf16),
                pltpu.VMEM((ROWS, FF), bf16),
                pltpu.VMEM((R, D), bf16),
                pltpu.VMEM((3, ROWS, TILE), bf16),
                pltpu.VMEM((R, HALF), f32),
                pltpu.VMEM((2, 128, HALF), f32),
                pltpu.VMEM((2, 64, HALF), f32),
                pltpu.VMEM((128, HALF), bf16),
                pltpu.VMEM((64, HALF), bf16),
                pltpu.VMEM((32, HALF), bf16),
                pltpu.VMEM((CHUNKS, 128, HALF), bf16),
                pltpu.VMEM((CHUNKS, 64, HALF), bf16),
                pltpu.VMEM((CHUNKS, 32, HALF), bf16),
                sem((3,)), sem((3, 2)), sem((3,)),
                sem((10, CHUNKS, 3)), sem((10, CHUNKS, 3)), pltpu.SemaphoreType.REGULAR((CHUNKS,)),
            ],
            compiler_params=pltpu.CompilerParams(collective_id=0, has_side_effects=True, vmem_limit_bytes=VMEM_LIMIT),
        )(*args))

    tokens, columns, rows = P("dp", None), P(None, "tp"), P("tp", None)
    return jax.shard_map(
        step,
        mesh=mesh,
        in_specs=(tokens, tokens, P("dp", "tp"), P("dp", "tp"), columns, columns, rows),
        out_specs=(tokens, P("dp", "tp"), P("dp", "tp"), P(("dp", "tp"), None)),
        check_vma=False,
    )


VMEM_LIMIT = 31_391_744
```

time: 284 us -> 172 us (0.61)
  Pallas kernels: 0 us -> 157 us
  matrix products: 134 us -> 0 us
  waiting for transfers between devices: 104 us -> 0 us
  local copies, waits for them, and re-layouts: 31.3 us -> 14.3 us
  between operations: 14 us -> 0.64 us
    pallas_call x0 -> x1, Pallas kernels: none -> 157 us  [step(): pl.pallas_call(kernel, out_shape=[pltpu.VMEM(s, bf16) for s in ((ROWS, D)...]
    dot_general x6 -> x0, matrix products: 134 us -> none  [the longest x1 26.2 us: step(): jnp.dot(d_up, w_up.T, preferred_element_type=jnp.float32)]
    psum x1 -> x0, waiting for transfers between devices: 104 us -> none  [step(): dx = lax.psum(term.astype(jnp.bfloat16), 'tp')]
    unnamed x5 -> x4, local copies, waits for them, and re-layouts: 31.3 us -> 14.3 us
  transfers between devices with their start and end apart: 1 -> 0, of which waited for: 1 -> 0; matrix products, arithmetic and copies ran while one was open for 28% -> 0% of each run, Pallas kernels for 0% -> 0%
where the time goes in v1:
time: 172 us
  Pallas kernels  157 us (91%)
  local copies, waits for them, and re-layouts  14.3 us (8%)
    pallas_call x1, Pallas kernels, step(): pl.pallas_call(kernel, out_shape=[pltpu.VMEM(s, bf16) for s in ((ROWS, D)...  157 us
    unnamed x4, local copies, waits for them, and re-layouts  14.3 us

profile of v1, /device:TPU:0, one launch (start us, length us, event | category | flops | bytes accessed | tf_op | source)
XLA Modules:
  0.0 171.8 jit_solution(6817189291162700418)
XLA Ops:
  0.6 156.9 %shard_map.102 = (bf16[2048,4096]{1,0:T(8,128)(2,1)S(1)}, bf16[4096,768]{1,0:T(8,128)(2,1)S(1)}, bf16[4096,768]{1,0:T(8,128)(2,1)S(1)}, bf16[768,4096]{1,0:T(8,128)(2,1)S(1)}) custom-call(bf16[2048,4096]{1,0:T(8,128)(2,1)} %x.1, bf16[2048,4096]{1,0:T(8,128)(2,1)} %dy.1, bf16[2048,768]{1,0:T(8,128)(2,1)} %gate.1, bf16[2048,768]{1,0:T(8,128)(2,1)} %up.1, ...), custom_call_target="tpu_custom_call" | custom-call | tf_op jit(solution)/shard_map/pallas_call | solution.py:320
  157.5 6.2 %copy.15 = bf16[2048,4096]{1,0:T(8,128)(2,1)} copy(bf16[2048,4096]{1,0:T(8,128)(2,1)S(1)} %get-tuple-element.4) | data formatting | bytes 33554432
  163.7 2.7 %copy.16 = bf16[4096,768]{1,0:T(8,128)(2,1)} copy(bf16[4096,768]{1,0:T(8,128)(2,1)S(1)} %get-tuple-element.5) | data formatting | bytes 12582912
  166.4 2.7 %copy.17 = bf16[4096,768]{1,0:T(8,128)(2,1)} copy(bf16[4096,768]{1,0:T(8,128)(2,1)S(1)} %get-tuple-element.6) | data formatting | bytes 12582912
  169.1 2.7 %copy.18 = bf16[768,4096]{1,0:T(8,128)(2,1)} copy(bf16[768,4096]{1,0:T(8,128)(2,1)S(1)} %get-tuple-element.7) | data formatting | bytes 12582912

commit v2 on v1

v2 whole, which is shorter than its diff:
```python
import jax
import jax.numpy as jnp
from jax import lax
from jax.experimental import pallas as pl
from jax.experimental.pallas import tpu as pltpu
from jax.sharding import PartitionSpec as P

bf16, f32 = jnp.bfloat16, jnp.float32
MESH = pl.DeviceIdType.MESH
ROWS, D, FF = 2048, 4096, 768
CHUNKS, R = 8, 256
HALF = D // 2
OFF, WIDTH = (0, 768, 1536), (768, 768, 512)
GROUPS = range(3)
TILE = 256
STRIP = 16
NB = 1024
KEPT = 4
PHASE1 = {
    (2, "b"): [("rs1", 0)],
    (2, "o"): [("rs1", 1)],
    (3, "b"): [("rs2", 0)],
    (3, "o"): [("rs1", 2)],
    (4, "b"): [("rs2", 1), ("rs3", 0)],
    (4, "o"): [("rs1", 3)],
    (5, "b"): [("rs3", 1), ("rs2", 2)],
    (5, "g"): [("ag3", 0)],
    (5, "o"): [("rs1", 4)],
    (6, "b"): [("rs2", 3), ("ag3", 1)],
    (6, "g"): [("rs3", 2)],
    (6, "o"): [("ag2", 0)],
    (7, "b"): [("rs1", 5)],
    (7, "o"): [("rs3", 3), ("rs2", 4)],
}
PHASE2 = {
    (0, "a"): [("ag3", 2), ("ag2", 1)],
    (1, "a"): [("rs1", 6), ("ag1", 0)],
    (3, "a"): [("rs2", 5)],
    (3, "b"): [("ag3", 3)],
    (4, "a"): [("rs3", 4)],
    (4, "b"): [("ag2", 2)],
    (6, "a"): [("rs1", 7), ("ag1", 1)],
    (6, "b"): [("rs2", 6)],
    (7, "a"): [("rs3", 5)],
    (7, "b"): [("ag2", 3)],
    (8, "a"): [("ag3", 4)],
    (9, "a"): [("rs2", 7), ("ag1", 2)],
    (9, "b"): [("rs3", 6)],
    (10, "a"): [("ag3", 5)],
    (11, "a"): [("ag1", 3)],
    (11, "b"): [("ag2", 4)],
    (12, "a"): [("rs3", 7), ("ag3", 6)],
    (13, "a"): [("ag2", 5)],
    (14, "a"): [("ag1", 4)],
    (14, "b"): [("ag3", 7)],
    (15, "a"): [("ag2", 6)],
}
LAST = [("ag1", 5), ("ag2", 7), ("ag1", 6), ("ag1", 7)]


def dot(a, b, ca, cb):
    return lax.dot_general(a, b, (((ca,), (cb,)), ((), ())), preferred_element_type=f32)


def kernel(
    x, dy, gate, up, wg, wu, wd,
    dx, dwg, dwu, dwd,
    dg, du, hid, dyb, ring, acc, kp1, kp2, s1, s2, s3, r1,
    dy_sem, w_sem, xd_sem, ss, rs, free,
):
    me = lax.axis_index("tp")
    core = lax.rem(me, 2)
    bits = tuple(lax.rem(me // s, 2) for s in (8, 4, 2))
    other = me + 1 - 2 * core

    def pick(r, values):
        return jnp.where(r == 0, values[0], jnp.where(r == 1, values[1], values[2]))

    peers = tuple(me + s * (1 - 2 * b) for s, b in zip((8, 4, 2), bits))

    def chunk_copies(k):
        rows = pl.ds(pl.multiple_of(k * R, R), R)
        return [
            pltpu.make_async_copy(dy.at[rows, :], dyb, dy_sem.at[0]),
            pltpu.make_async_copy(gate.at[rows, :], hid.at[rows, :], dy_sem.at[1]),
            pltpu.make_async_copy(up.at[rows, :], du.at[rows, :], dy_sem.at[2]),
        ]

    def w_copies(half, i):
        rows = pl.ds(pl.multiple_of(half * HALF, HALF), HALF)
        return [pltpu.make_async_copy(a.at[rows, :], b.at[rows, :], w_sem.at[i, n]) for n, (a, b) in enumerate(((wg, dwg), (wu, dwu)))]

    def xd_copy(t, which):
        i = 2 * t + which
        cols = pl.ds(pl.multiple_of(t * TILE, TILE), TILE)
        return pltpu.make_async_copy((x, dy)[which].at[:, cols], ring.at[lax.rem(i, 3)], xd_sem.at[lax.rem(i, 3)])

    wd_copy = pltpu.make_async_copy(wd, dwd, w_sem.at[2, 0])
    first = chunk_copies(0)
    first[0].start()
    wd_copy.start()
    first[1].start()
    first[2].start()
    for c in w_copies(1 - core, 0) + w_copies(core, 1):
        c.start()

    barrier = pltpu.get_barrier_semaphore()
    for p in peers + (other,):
        pl.semaphore_signal(barrier, inc=1, device_id={"tp": p}, device_id_type=MESH)
    pl.semaphore_wait(barrier, 4)

    def remote(kind, k, g, src, dst, to):
        return pltpu.make_async_remote_copy(
            src_ref=src, dst_ref=dst, send_sem=ss.at[kind, k, g], recv_sem=rs.at[kind, k, g],
            device_id={"tp": to}, device_id_type=MESH,
        )

    def place(k, g):
        o = [lax.rem(g + k + i, 3) for i in range(3)]
        b = [pick(r, bits) for r in o]
        p = [pick(r, peers) for r in o]
        keep1 = k * R + b[0] * 128
        send1 = k * R + (1 - b[0]) * 128
        keep2, send2 = keep1 + b[1] * 64, keep1 + (1 - b[1]) * 64
        keep3, send3 = keep2 + b[2] * 32, keep2 + (1 - b[2]) * 32
        return b, p, (keep1, keep2, keep3), (send1, send2, send3)

    def mine(start, n, g):
        return dx.at[pl.ds(pl.multiple_of(start, STRIP), n), pl.ds(pl.multiple_of(core * HALF + OFF[g], 256), WIDTH[g])]

    def theirs(k, g):
        return dx.at[pl.ds(pl.multiple_of(k * R, R), R), pl.ds(pl.multiple_of((1 - core) * HALF + OFF[g], 256), WIDTH[g])]

    def copy_of(kind, k, g):
        b, p, keep, send = place(k, g)
        cols = pl.ds(OFF[g], WIDTH[g])
        if kind == 0:
            return remote(0, k, g, theirs(k, g), theirs(k, g), other)
        if kind == 1:
            return remote(1, k, g, s1.at[:, cols], r1.at[k, :, cols], p[0])
        if kind == 2:
            there = keep[0] + (1 - b[1]) * 64
            return remote(2, k, g, s2.at[:, cols], mine(there, 64, g), p[1])
        if kind == 3:
            return remote(3, k, g, s3.at[:, cols], r1.at[k, pl.ds(0, 32), cols], p[2])
        if kind == 4:
            return remote(4, k, g, mine(keep[2], 32, g), mine(keep[2], 32, g), p[2])
        if kind == 5:
            return remote(5, k, g, mine(keep[1], 64, g), mine(keep[1], 64, g), p[1])
        if kind == 6:
            return remote(6, k, g, mine(keep[0], 128, g), mine(keep[0], 128, g), p[0])
        if kind == 7:
            return remote(7, k, g, mine(keep[1], 64, g), mine(keep[1], 64, g), other)
        if kind == 8:
            return remote(8, k, g, mine(send[1], 64, g), mine(send[1], 64, g), other)
        return remote(9, k, g, mine(send[0], 128, g), mine(send[0], 128, g), other)

    def part(start, i):
        return pl.ds(pl.multiple_of(start + i, STRIP), STRIP)

    def event(kind, k, work=None, after=()):
        for g in GROUPS:
            copy_of(kind, k, g).wait_recv()
        if kind < 3 and k > 0:
            for g in GROUPS:
                copy_of(kind + 1, k - 1, g).wait_send()
        if work is not None:
            for g in GROUPS:
                work(k, g, pl.ds(OFF[g], WIDTH[g]), *place(k, g))
        for g in GROUPS:
            for n in after:
                copy_of(n, k, g).start()

    def own(k):
        for g in GROUPS:
            copy_of(0, k, g).wait_recv()

        @pl.when(k >= 1)
        def _():
            for g in GROUPS:
                copy_of(1, k - 1, g).wait_send()

        for g in GROUPS:
            b, p, keep, send = place(k, g)
            cols = pl.ds(OFF[g], WIDTH[g])
            for i in range(0, 128, STRIP):
                v = acc[part((1 - b[0]) * 128, i), cols] + mine(send[0] + i, STRIP, g)[...].astype(f32)
                s1[pl.ds(i, STRIP), cols] = v.astype(bf16)
                v = acc[part(b[0] * 128, i), cols] + mine(keep[0] + i, STRIP, g)[...].astype(f32)
                kp1[lax.rem(k, 2), pl.ds(i, STRIP), cols] = v
        for g in GROUPS:
            copy_of(1, k, g).start()

    def halve1(k, g, cols, b, p, keep, send):
        for i in range(0, 64, STRIP):
            rows = part((1 - b[1]) * 64, i)
            s2[pl.ds(i, STRIP), cols] = (kp1[k % 2, rows, cols] + r1[k, rows, cols].astype(f32)).astype(bf16)
            rows = part(b[1] * 64, i)
            kp2[k % KEPT, pl.ds(i, STRIP), cols] = kp1[k % 2, rows, cols] + r1[k, rows, cols].astype(f32)

    def halve2(k, g, cols, b, p, keep, send):
        for i in range(0, 32, STRIP):
            v = kp2[k % KEPT, part((1 - b[2]) * 32, i), cols] + mine(send[2] + i, STRIP, g)[...].astype(f32)
            s3[pl.ds(i, STRIP), cols] = v.astype(bf16)
            rows = part(b[2] * 32, i)
            kp2[k % KEPT, rows, cols] = kp2[k % KEPT, rows, cols] + mine(keep[2] + i, STRIP, g)[...].astype(f32)

    def halve3(k, g, cols, b, p, keep, send):
        for i in range(0, 32, STRIP):
            v = kp2[k % KEPT, part(b[2] * 32, i), cols] + r1[k, pl.ds(i, STRIP), cols].astype(f32)
            mine(keep[2] + i, STRIP, g)[...] = v.astype(bf16)

    def gather3(k):
        pl.semaphore_wait(free.at[k], 1)
        event(4, k, after=(5, 7))

    EVENTS = {
        "rs1": lambda k: event(1, k, halve1, (2,)),
        "rs2": lambda k: event(2, k, halve2, (3,)),
        "rs3": lambda k: event(3, k, halve3, (4,)),
        "ag3": gather3,
        "ag2": lambda k: event(5, k, after=(6, 8)),
        "ag1": lambda k: event(6, k, after=(9,)),
    }

    def exchanges(step, table, point):
        for (n, at), events in table.items():
            if at == point:
                @pl.when(step == n)
                def _():
                    for name, k in events:
                        EVENTS[name](k)

    def gradients(k):
        for c in chunk_copies(k):
            c.wait()
        acc[:, pl.ds(0, FF)] = dot(dyb[...], dwd[...], 1, 1)
        @pl.loop(0, R // 32)
        def _(n):
            i = pl.multiple_of(n * 32, 32)
            here = pl.ds(pl.multiple_of(k * R + i, 32), 32)
            a, b, d = hid[here, :].astype(f32), du[here, :].astype(f32), acc[pl.ds(i, 32), pl.ds(0, FF)]
            sig = jax.nn.sigmoid(a)
            silu = a * sig
            hid[here, :] = (silu * b).astype(bf16)
            du[here, :] = (d * silu).astype(bf16)
            dg[here, :] = (d * b * (sig + silu * (1.0 - sig))).astype(bf16)

    def term(k, half):
        rows = pl.ds(pl.multiple_of(k * R, R), R)
        @pl.loop(0, HALF // NB)
        def _(j):
            n = pl.multiple_of(j * NB, NB)
            w = pl.ds(pl.multiple_of(half * HALF + n, 256), NB)
            acc[:, pl.ds(n, NB)] = dot(dg[rows, :], dwg[w, :], 1, 1) + dot(du[rows, :], dwu[w, :], 1, 1)

    wd_copy.wait()
    gradients(0)
    for c in chunk_copies(1):
        c.start()
    for c in w_copies(1 - core, 0):
        c.wait()

    @pl.loop(0, CHUNKS)
    def _(k):
        term(k, 1 - core)
        for g in GROUPS:
            ref = theirs(k, g)
            for i in range(0, R, 32):
                ref[pl.ds(i, 32), :] = acc[pl.ds(i, 32), pl.ds(OFF[g], WIDTH[g])].astype(bf16)
        for g in GROUPS:
            copy_of(0, k, g).start()
        exchanges(k, PHASE1, "b")

        @pl.when(k < CHUNKS - 1)
        def _():
            gradients(k + 1)

        @pl.when(k < CHUNKS - 2)
        def _():
            for c in chunk_copies(k + 2):
                c.start()

        @pl.when(k == CHUNKS - 2)
        def _():
            for i in range(3):
                xd_copy(i // 2, i % 2).start()

        exchanges(k, PHASE1, "g")

        @pl.when(k == 0)
        def _():
            for c in w_copies(core, 1):
                c.wait()

        term(k, core)
        own(k)
        for g in GROUPS:
            copy_of(0, k, g).wait_send()
        pl.semaphore_signal(free.at[k], inc=1, device_id={"tp": other}, device_id_type=MESH)
        exchanges(k, PHASE1, "o")

    @pl.loop(0, 16)
    def _(t):
        tile = pl.ds(pl.multiple_of(t * TILE, TILE), TILE)
        xd_copy(t, 0).wait()
        xd_copy(t, 1).wait()
        xt, yt = ring.at[lax.rem(2 * t, 3)], ring.at[lax.rem(2 * t + 1, 3)]
        dwg[tile, :] = dot(xt[...], dg[...], 0, 0).astype(bf16)
        dwu[tile, :] = dot(xt[...], du[...], 0, 0).astype(bf16)

        @pl.when(t < 15)
        def _():
            xd_copy(t + 1, 1).start()

        exchanges(t, PHASE2, "a")
        dwd[:, tile] = dot(hid[...], yt[...], 0, 0).astype(bf16)

        @pl.when(t < 14)
        def _():
            xd_copy(t + 2, 0).start()

        exchanges(t, PHASE2, "b")

    for name, k in LAST:
        EVENTS[name](k)

    @pl.loop(0, CHUNKS)
    def _(k):
        for g in GROUPS:
            for kind in range(4, 10):
                if kind >= 7:
                    copy_of(kind, k, g).wait_recv()
                copy_of(kind, k, g).wait_send()

    for g in GROUPS:
        for kind in range(1, 4):
            copy_of(kind, CHUNKS - 1, g).wait_send()


def solution(mesh):
    hbm = pl.BlockSpec(memory_space=pltpu.HBM)
    vmem = pl.BlockSpec(memory_space=pltpu.VMEM)
    sem = pltpu.SemaphoreType.DMA

    def step(*args):
        return tuple(pl.pallas_call(
            kernel,
            out_shape=[pltpu.VMEM(s, bf16) for s in ((ROWS, D), (D, FF), (D, FF), (FF, D))],
            in_specs=[hbm] * 7,
            out_specs=[vmem] * 4,
            scratch_shapes=[
                pltpu.VMEM((ROWS, FF), bf16),
                pltpu.VMEM((ROWS, FF), bf16),
                pltpu.VMEM((ROWS, FF), bf16),
                pltpu.VMEM((R, D), bf16),
                pltpu.VMEM((3, ROWS, TILE), bf16),
                pltpu.VMEM((R, HALF), f32),
                pltpu.VMEM((2, 128, HALF), f32),
                pltpu.VMEM((4, 64, HALF), f32),
                pltpu.VMEM((128, HALF), bf16),
                pltpu.VMEM((64, HALF), bf16),
                pltpu.VMEM((32, HALF), bf16),
                pltpu.VMEM((CHUNKS, 128, HALF), bf16),
                sem((3,)), sem((3, 2)), sem((3,)),
                sem((10, CHUNKS, 3)), sem((10, CHUNKS, 3)), pltpu.SemaphoreType.REGULAR((CHUNKS,)),
            ],
            compiler_params=pltpu.CompilerParams(collective_id=0, has_side_effects=True, vmem_limit_bytes=VMEM_LIMIT),
        )(*args))

    tokens, columns, rows = P("dp", None), P(None, "tp"), P("tp", None)
    return jax.shard_map(
        step,
        mesh=mesh,
        in_specs=(tokens, tokens, P("dp", "tp"), P("dp", "tp"), columns, columns, rows),
        out_specs=(tokens, P("dp", "tp"), P("dp", "tp"), P(("dp", "tp"), None)),
        check_vma=False,
    )


VMEM_LIMIT = 31_391_744
```

time: 172 us -> 152 us (0.88)
  Pallas kernels: 157 us -> 137 us
    pallas_call x1, Pallas kernels: 157 us -> 137 us  [step(): pl.pallas_call(kernel, out_shape=[pltpu.VMEM(s, bf16) for s in ((ROWS, D)...]
where the time goes in v2:
time: 152 us; the launch traced here: 151 us
  Pallas kernels  137 us (90%)
  local copies, waits for them, and re-layouts  14.3 us (9%)
    pallas_call x1, Pallas kernels, step(): pl.pallas_call(kernel, out_shape=[pltpu.VMEM(s, bf16) for s in ((ROWS, D)...  137 us
    unnamed x4, local copies, waits for them, and re-layouts  14.3 us

profile of v2, /device:TPU:0, one launch (start us, length us, event | category | flops | bytes accessed | tf_op | source)
XLA Modules:
  0.0 151.5 jit_solution(14886608056822074031)
XLA Ops:
  0.6 136.6 %shard_map.102 = (bf16[2048,4096]{1,0:T(8,128)(2,1)S(1)}, bf16[4096,768]{1,0:T(8,128)(2,1)S(1)}, bf16[4096,768]{1,0:T(8,128)(2,1)S(1)}, bf16[768,4096]{1,0:T(8,128)(2,1)S(1)}) custom-call(bf16[2048,4096]{1,0:T(8,128)(2,1)} %x.1, bf16[2048,4096]{1,0:T(8,128)(2,1)} %dy.1, bf16[2048,768]{1,0:T(8,128)(2,1)} %gate.1, bf16[2048,768]{1,0:T(8,128)(2,1)} %up.1, ...), custom_call_target="tpu_custom_call" | custom-call | tf_op jit(solution)/shard_map/pallas_call | solution.py:347
  137.2 6.2 %copy.15 = bf16[2048,4096]{1,0:T(8,128)(2,1)} copy(bf16[2048,4096]{1,0:T(8,128)(2,1)S(1)} %get-tuple-element.4) | data formatting | bytes 33554432
  143.4 2.7 %copy.16 = bf16[4096,768]{1,0:T(8,128)(2,1)} copy(bf16[4096,768]{1,0:T(8,128)(2,1)S(1)} %get-tuple-element.5) | data formatting | bytes 12582912
  146.1 2.7 %copy.17 = bf16[4096,768]{1,0:T(8,128)(2,1)} copy(bf16[4096,768]{1,0:T(8,128)(2,1)S(1)} %get-tuple-element.6) | data formatting | bytes 12582912
  148.8 2.7 %copy.18 = bf16[768,4096]{1,0:T(8,128)(2,1)} copy(bf16[768,4096]{1,0:T(8,128)(2,1)S(1)} %get-tuple-element.7) | data formatting | bytes 12582912

commit v3 on v2

--- a/solution.py
+++ b/solution.py
@@ -17,45 +17,44 @@
 NB = 1024
 KEPT = 4
 PHASE1 = {
-    (2, "b"): [("rs1", 0)],
+    (1, "o"): [("rs1", 0)],
     (2, "o"): [("rs1", 1)],
     (3, "b"): [("rs2", 0)],
     (3, "o"): [("rs1", 2)],
-    (4, "b"): [("rs2", 1), ("rs3", 0)],
+    (4, "b"): [("rs3", 0), ("rs2", 1)],
     (4, "o"): [("rs1", 3)],
-    (5, "b"): [("rs3", 1), ("rs2", 2)],
-    (5, "g"): [("ag3", 0)],
+    (5, "b"): [("rs2", 2), ("ag3", 0)],
+    (5, "g"): [("rs3", 1)],
     (5, "o"): [("rs1", 4)],
-    (6, "b"): [("rs2", 3), ("ag3", 1)],
-    (6, "g"): [("rs3", 2)],
-    (6, "o"): [("ag2", 0)],
+    (6, "b"): [("rs2", 3), ("rs3", 2)],
+    (6, "g"): [("ag2", 0)],
+    (6, "o"): [("ag3", 1)],
     (7, "b"): [("rs1", 5)],
     (7, "o"): [("rs3", 3), ("rs2", 4)],
 }
 PHASE2 = {
-    (0, "a"): [("ag3", 2), ("ag2", 1)],
-    (1, "a"): [("rs1", 6), ("ag1", 0)],
-    (3, "a"): [("rs2", 5)],
-    (3, "b"): [("ag3", 3)],
-    (4, "a"): [("rs3", 4)],
-    (4, "b"): [("ag2", 2)],
-    (6, "a"): [("rs1", 7), ("ag1", 1)],
-    (6, "b"): [("rs2", 6)],
-    (7, "a"): [("rs3", 5)],
-    (7, "b"): [("ag2", 3)],
-    (8, "a"): [("ag3", 4)],
-    (9, "a"): [("rs2", 7), ("ag1", 2)],
-    (9, "b"): [("rs3", 6)],
-    (10, "a"): [("ag3", 5)],
-    (11, "a"): [("ag1", 3)],
-    (11, "b"): [("ag2", 4)],
-    (12, "a"): [("rs3", 7), ("ag3", 6)],
-    (13, "a"): [("ag2", 5)],
-    (14, "a"): [("ag1", 4)],
-    (14, "b"): [("ag3", 7)],
-    (15, "a"): [("ag2", 6)],
+    (0, "a"): [("ag3", 2), ("ag1", 0)],
+    (0, "b"): [("rs1", 6), ("ag2", 1)],
+    (2, "b"): [("rs2", 5)],
+    (3, "a"): [("rs3", 4), ("ag3", 3)],
+    (4, "a"): [("rs1", 7), ("ag2", 2)],
+    (5, "b"): [("rs2", 6)],
+    (6, "a"): [("rs3", 5), ("ag1", 1)],
+    (6, "b"): [("ag3", 4)],
+    (7, "a"): [("ag2", 3)],
+    (8, "a"): [("rs2", 7)],
+    (8, "b"): [("ag1", 2)],
+    (9, "a"): [("rs3", 6), ("ag3", 5)],
+    (10, "a"): [("ag2", 4)],
+    (11, "a"): [("ag1", 3), ("rs3", 7)],
+    (11, "b"): [("ag3", 6)],
+    (12, "a"): [("ag2", 5)],
+    (13, "b"): [("ag1", 4)],
+    (14, "a"): [("ag3", 7)],
+    (14, "b"): [("ag2", 6)],
+    (15, "b"): [("ag1", 5)],
 }
-LAST = [("ag1", 5), ("ag2", 7), ("ag1", 6), ("ag1", 7)]
+LAST = [("ag2", 7), ("ag1", 6), ("ag1", 7)]
 
 
 def dot(a, b, ca, cb):
@@ -66,7 +65,7 @@
     x, dy, gate, up, wg, wu, wd,
     dx, dwg, dwu, dwd,
     dg, du, hid, dyb, ring, acc, kp1, kp2, s1, s2, s3, r1,
-    dy_sem, w_sem, xd_sem, ss, rs, free,
+    dy_sem, wd_sem, w_sem, xd_sem, ss, rs, free,
 ):
     me = lax.axis_index("tp")
     core = lax.rem(me, 2)
@@ -86,24 +85,26 @@
             pltpu.make_async_copy(up.at[rows, :], du.at[rows, :], dy_sem.at[2]),
         ]
 
-    def w_copies(half, i):
-        rows = pl.ds(pl.multiple_of(half * HALF, HALF), HALF)
-        return [pltpu.make_async_copy(a.at[rows, :], b.at[rows, :], w_sem.at[i, n]) for n, (a, b) in enumerate(((wg, dwg), (wu, dwu)))]
+    def w_copies(half, j):
+        rows = pl.ds(pl.multiple_of(half * HALF + j * NB, NB), NB)
+        where = half * (HALF // NB) + j
+        return [pltpu.make_async_copy(a.at[rows, :], b.at[rows, :], w_sem.at[where, n]) for n, (a, b) in enumerate(((wg, dwg), (wu, dwu)))]
 
     def xd_copy(t, which):
         i = 2 * t + which
         cols = pl.ds(pl.multiple_of(t * TILE, TILE), TILE)
         return pltpu.make_async_copy((x, dy)[which].at[:, cols], ring.at[lax.rem(i, 3)], xd_sem.at[lax.rem(i, 3)])
 
-    wd_copy = pltpu.make_async_copy(wd, dwd, w_sem.at[2, 0])
+    def wd_copy(n):
+        rows = pl.ds(n * TILE, TILE)
+        return pltpu.make_async_copy(wd.at[rows, :], dwd.at[rows, :], wd_sem.at[n])
+
     first = chunk_copies(0)
     first[0].start()
-    wd_copy.start()
+    for n in range(3):
+        wd_copy(n).start()
     first[1].start()
     first[2].start()
-    for c in w_copies(1 - core, 0) + w_copies(core, 1):
-        c.start()
-
     barrier = pltpu.get_barrier_semaphore()
     for p in peers + (other,):
         pl.semaphore_signal(barrier, inc=1, device_id={"tp": p}, device_id_type=MESH)
@@ -232,14 +233,23 @@
                         EVENTS[name](k)
 
     def gradients(k):
-        for c in chunk_copies(k):
-            c.wait()
-        acc[:, pl.ds(0, FF)] = dot(dyb[...], dwd[...], 1, 1)
-        @pl.loop(0, R // 32)
+        copies = chunk_copies(k)
+        copies[0].wait()
+        if isinstance(k, int) and k == 0:
+            for n in range(3):
+                wd_copy(n).wait()
+                cols = pl.ds(n * TILE, TILE)
+                acc[:, cols] = dot(dyb[...], dwd[cols, :], 1, 1)
+        else:
+            acc[:, pl.ds(0, FF)] = dot(dyb[...], dwd[...], 1, 1)
+        copies[1].wait()
+        copies[2].wait()
+
+        @pl.loop(0, R // 16, unroll=2)
         def _(n):
-            i = pl.multiple_of(n * 32, 32)
-            here = pl.ds(pl.multiple_of(k * R + i, 32), 32)
-            a, b, d = hid[here, :].astype(f32), du[here, :].astype(f32), acc[pl.ds(i, 32), pl.ds(0, FF)]
+            i = pl.multiple_of(n * 16, 16)
+            here = pl.ds(pl.multiple_of(k * R + i, 16), 16)
+            a, b, d = hid[here, :].astype(f32), du[here, :].astype(f32), acc[pl.ds(i, 16), pl.ds(0, FF)]
             sig = jax.nn.sigmoid(a)
             silu = a * sig
             hid[here, :] = (silu * b).astype(bf16)
@@ -250,25 +260,31 @@
         rows = pl.ds(pl.multiple_of(k * R, R), R)
         @pl.loop(0, HALF // NB)
         def _(j):
+            @pl.when(k == 0)
+            def _():
+                for c in w_copies(half, j):
+                    c.wait()
+
             n = pl.multiple_of(j * NB, NB)
             w = pl.ds(pl.multiple_of(half * HALF + n, 256), NB)
-            acc[:, pl.ds(n, NB)] = dot(dg[rows, :], dwg[w, :], 1, 1) + dot(du[rows, :], dwu[w, :], 1, 1)
-
-    wd_copy.wait()
+            t = dot(dg[rows, :], dwg[w, :], 1, 1) + dot(du[rows, :], dwu[w, :], 1, 1)
+            if half is core:
+                acc[:, pl.ds(n, NB)] = t
+            else:
+                dx[rows, w] = t.astype(bf16)
+
+    for half in (1 - core, core):
+        for j in range(HALF // NB):
+            for c in w_copies(half, j):
+                c.start()
     gradients(0)
     for c in chunk_copies(1):
         c.start()
-    for c in w_copies(1 - core, 0):
-        c.wait()
 
     @pl.loop(0, CHUNKS)
     def _(k):
         term(k, 1 - core)
         for g in GROUPS:
-            ref = theirs(k, g)
-            for i in range(0, R, 32):
-                ref[pl.ds(i, 32), :] = acc[pl.ds(i, 32), pl.ds(OFF[g], WIDTH[g])].astype(bf16)
-        for g in GROUPS:
             copy_of(0, k, g).start()
         exchanges(k, PHASE1, "b")
 
@@ -287,11 +303,6 @@
                 xd_copy(i // 2, i % 2).start()
 
         exchanges(k, PHASE1, "g")
-
-        @pl.when(k == 0)
-        def _():
-            for c in w_copies(core, 1):
-                c.wait()
 
         term(k, core)
         own(k)
@@ -338,13 +349,38 @@
             copy_of(kind, CHUNKS - 1, g).wait_send()
 
 
+def write_out(*arrays):
+    n = len(arrays)
+
+    def copies(*refs):
+        out = [
+            pltpu.make_async_copy(a.at[rows], b.at[rows], refs[-1].at[4 * i + q])
+            for i, (a, b) in enumerate(zip(refs[:n], refs[n : 2 * n]))
+            for q in range(4)
+            for rows in [pl.ds(q * (a.shape[0] // 4), a.shape[0] // 4)]
+        ]
+        for c in out:
+            c.start()
+        for c in out:
+            c.wait()
+
+    return pl.pallas_call(
+        copies,
+        out_shape=[jax.ShapeDtypeStruct(a.shape, a.dtype) for a in arrays],
+        in_specs=[pl.BlockSpec(memory_space=pltpu.VMEM)] * n,
+        out_specs=[pl.BlockSpec(memory_space=pl.ANY)] * n,
+        scratch_shapes=[pltpu.SemaphoreType.DMA((4 * n,))],
+        compiler_params=pltpu.CompilerParams(vmem_limit_bytes=1024),
+    )(*arrays)
+
+
 def solution(mesh):
     hbm = pl.BlockSpec(memory_space=pltpu.HBM)
     vmem = pl.BlockSpec(memory_space=pltpu.VMEM)
     sem = pltpu.SemaphoreType.DMA
 
     def step(*args):
-        return tuple(pl.pallas_call(
+        dx, *dw = pl.pallas_call(
             kernel,
             out_shape=[pltpu.VMEM(s, bf16) for s in ((ROWS, D), (D, FF), (D, FF), (FF, D))],
             in_specs=[hbm] * 7,
@@ -362,11 +398,12 @@
                 pltpu.VMEM((64, HALF), bf16),
                 pltpu.VMEM((32, HALF), bf16),
                 pltpu.VMEM((CHUNKS, 128, HALF), bf16),
-                sem((3,)), sem((3, 2)), sem((3,)),
+                sem((3,)), sem((3,)), sem((D // NB, 2)), sem((3,)),
                 sem((10, CHUNKS, 3)), sem((10, CHUNKS, 3)), pltpu.SemaphoreType.REGULAR((CHUNKS,)),
             ],
             compiler_params=pltpu.CompilerParams(collective_id=0, has_side_effects=True, vmem_limit_bytes=VMEM_LIMIT),
-        )(*args))
+        )(*args)
+        return (*write_out(dx), *write_out(*dw))
 
     tokens, columns, rows = P("dp", None), P(None, "tp"), P("tp", None)
     return jax.shard_map(

time: 152 us -> 147 us (0.967)
  local copies, waits for them, and re-layouts: 14.3 us -> 0 us
  Pallas kernels: 137 us -> 146 us
    unnamed x4 -> x0, local copies, waits for them, and re-layouts: 14.3 us -> none
    pallas_call x0 -> x2, Pallas kernels: none -> 12.5 us  [write_out(): pl.pallas_call(copies, out_shape=[jax.ShapeDtypeStruct(a.shape, a.dtype)...]
    pallas_call x1, Pallas kernels: 137 us -> 134 us  [step(): pl.pallas_call(kernel, out_shape=[pltpu.VMEM(s, bf16) for s in ((ROWS, D)...]
where the time goes in v3:
time: 147 us
  Pallas kernels  146 us (99%)
    pallas_call x1, Pallas kernels, step(): pl.pallas_call(kernel, out_shape=[pltpu.VMEM(s, bf16) for s in ((ROWS, D)...  134 us
    pallas_call x2, Pallas kernels, write_out(): pl.pallas_call(copies, out_shape=[jax.ShapeDtypeStruct(a.shape, a.dtype)...  12.5 us

profile of v3, /device:TPU:0, one launch (start us, length us, event | category | flops | bytes accessed | tf_op | source)
XLA Modules:
  0.0 146.8 jit_solution(15507963759499869600)
XLA Ops:
  0.6 133.6 %shard_map.102 = (bf16[2048,4096]{1,0:T(8,128)(2,1)S(1)}, bf16[4096,768]{1,0:T(8,128)(2,1)S(1)}, bf16[4096,768]{1,0:T(8,128)(2,1)S(1)}, bf16[768,4096]{1,0:T(8,128)(2,1)S(1)}) custom-call(bf16[2048,4096]{1,0:T(8,128)(2,1)} %x.1, bf16[2048,4096]{1,0:T(8,128)(2,1)} %dy.1, bf16[2048,768]{1,0:T(8,128)(2,1)} %gate.1, bf16[2048,768]{1,0:T(8,128)(2,1)} %up.1, ...), custom_call_target="tpu_custom_call" | custom-call | tf_op jit(solution)/shard_map/pallas_call | solution.py:383
  134.3 6.0 %shard_map.103 = bf16[2048,4096]{1,0:T(8,128)(2,1)} custom-call(bf16[2048,4096]{1,0:T(8,128)(2,1)S(1)} %get-tuple-element.11.refs_0_), custom_call_target="tpu_custom_call" | custom-call | tf_op jit(solution)/shard_map/pallas_call | solution.py:367
  140.2 6.6 %shard_map.104 = (bf16[4096,768]{1,0:T(8,128)(2,1)}, bf16[4096,768]{1,0:T(8,128)(2,1)}, bf16[768,4096]{1,0:T(8,128)(2,1)}) custom-call(bf16[4096,768]{1,0:T(8,128)(2,1)S(1)} %get-tuple-element.12.refs_0_, bf16[4096,768]{1,0:T(8,128)(2,1)S(1)} %get-tuple-element.13.refs_1_, bf16[768,4096]{1,0:T(8,128)(2,1)S(1)} %get-tuple-element.14.refs_2_), custom_call_target="tpu_custom_call" | custom-call | tf_op jit(solution)/shard_map/pallas_call | solution.py:367

commit v4 on v3

--- a/solution.py
+++ b/solution.py
@@ -333,31 +333,40 @@
 
         exchanges(t, PHASE2, "b")
 
-    for name, k in LAST:
-        EVENTS[name](k)
-
-    @pl.loop(0, CHUNKS)
-    def _(k):
+    def finish(k):
         for g in GROUPS:
             for kind in range(4, 10):
                 if kind >= 7:
                     copy_of(kind, k, g).wait_recv()
                 copy_of(kind, k, g).wait_send()
 
+    first = 1 + max(i for i, (name, _) in enumerate(LAST) if name != "ag1")
+    for name, k in LAST[:first]:
+        EVENTS[name](k)
     for g in GROUPS:
         for kind in range(1, 4):
             copy_of(kind, CHUNKS - 1, g).wait_send()
 
+    @pl.loop(0, min(k for name, k in LAST if name == "ag1"))
+    def _(k):
+        finish(k)
+
+    for name, k in LAST[first:]:
+        EVENTS[name](k)
+    for name, k in LAST:
+        if name == "ag1":
+            finish(k)
+
 
 def write_out(*arrays):
     n = len(arrays)
 
     def copies(*refs):
         out = [
-            pltpu.make_async_copy(a.at[rows], b.at[rows], refs[-1].at[4 * i + q])
+            pltpu.make_async_copy(a.at[rows], b.at[rows], refs[-1].at[8 * i + q])
             for i, (a, b) in enumerate(zip(refs[:n], refs[n : 2 * n]))
-            for q in range(4)
-            for rows in [pl.ds(q * (a.shape[0] // 4), a.shape[0] // 4)]
+            for q in range(8)
+            for rows in [pl.ds(q * (a.shape[0] // 8), a.shape[0] // 8)]
         ]
         for c in out:
             c.start()
@@ -369,7 +378,7 @@
         out_shape=[jax.ShapeDtypeStruct(a.shape, a.dtype) for a in arrays],
         in_specs=[pl.BlockSpec(memory_space=pltpu.VMEM)] * n,
         out_specs=[pl.BlockSpec(memory_space=pl.ANY)] * n,
-        scratch_shapes=[pltpu.SemaphoreType.DMA((4 * n,))],
+        scratch_shapes=[pltpu.SemaphoreType.DMA((8 * n,))],
         compiler_params=pltpu.CompilerParams(vmem_limit_bytes=1024),
     )(*arrays)
 

time: 147 us -> 147 us (level)
  no operation moved by 1% of the time
where the time goes in v4:
time: 147 us
  Pallas kernels  146 us (99%)
    pallas_call x1, Pallas kernels, step(): pl.pallas_call(kernel, out_shape=[pltpu.VMEM(s, bf16) for s in ((ROWS, D)...  134 us
    pallas_call x2, Pallas kernels, write_out(): pl.pallas_call(copies, out_shape=[jax.ShapeDtypeStruct(a.shape, a.dtype)...  12.6 us

profile of v4, /device:TPU:0, one launch (start us, length us, event | category | flops | bytes accessed | tf_op | source)
XLA Modules:
  0.0 146.9 jit_solution(13236104978140056665)
XLA Ops:
  0.6 133.6 %shard_map.102 = (bf16[2048,4096]{1,0:T(8,128)(2,1)S(1)}, bf16[4096,768]{1,0:T(8,128)(2,1)S(1)}, bf16[4096,768]{1,0:T(8,128)(2,1)S(1)}, bf16[768,4096]{1,0:T(8,128)(2,1)S(1)}) custom-call(bf16[2048,4096]{1,0:T(8,128)(2,1)} %x.1, bf16[2048,4096]{1,0:T(8,128)(2,1)} %dy.1, bf16[2048,768]{1,0:T(8,128)(2,1)} %gate.1, bf16[2048,768]{1,0:T(8,128)(2,1)} %up.1, ...), custom_call_target="tpu_custom_call" | custom-call | tf_op jit(solution)/shard_map/pallas_call | solution.py:392
  134.3 5.9 %shard_map.103 = bf16[2048,4096]{1,0:T(8,128)(2,1)} custom-call(bf16[2048,4096]{1,0:T(8,128)(2,1)S(1)} %get-tuple-element.11.refs_0_), custom_call_target="tpu_custom_call" | custom-call | tf_op jit(solution)/shard_map/pallas_call | solution.py:376
  140.2 6.7 %shard_map.104 = (bf16[4096,768]{1,0:T(8,128)(2,1)}, bf16[4096,768]{1,0:T(8,128)(2,1)}, bf16[768,4096]{1,0:T(8,128)(2,1)}) custom-call(bf16[4096,768]{1,0:T(8,128)(2,1)S(1)} %get-tuple-element.12.refs_0_, bf16[4096,768]{1,0:T(8,128)(2,1)S(1)} %get-tuple-element.13.refs_1_, bf16[768,4096]{1,0:T(8,128)(2,1)S(1)} %get-tuple-element.14.refs_2_), custom_call_target="tpu_custom_call" | custom-call | tf_op jit(solution)/shard_map/pallas_call | solution.py:376
